TPU v7x, 128 devices: a whole 4x4x4 slice. The times are simulated.
128 devices in a mesh: batch: 1, graph: 128 (over z, y, x, core).
Axes of the slice: x: 4, y: 4, z: 4, core: 2. Of those that a mesh axis runs over, the one named last changes fastest.
Arguments:
- grid_in: float32 [65536, 186], P(('batch', 'graph'))
- mesh_in: float32 [32768, 3], P(('batch', 'graph'))
- edge_in: float32 [1048576, 4], P(('batch', 'graph'))
- edge_src: int32 [1048576], P(('batch', 'graph'))
- edge_dst: int32 [1048576], P(('batch', 'graph'))
- edge_mask: int32 [1048576], P(('batch', 'graph'))
- grid_w1: bfloat16 [186, 512], replicated
- grid_w2: bfloat16 [512, 512], replicated
- grid_vec: float32 [4, 512], replicated
- mesh_w1: bfloat16 [3, 512], replicated
- mesh_w2: bfloat16 [512, 512], replicated
- mesh_vec: float32 [4, 512], replicated
- embed_w1: bfloat16 [4, 512], replicated
- embed_w2: bfloat16 [512, 512], replicated
- embed_vec: float32 [4, 512], replicated
- edge_w1: bfloat16 [1536, 512], replicated
- edge_w2: bfloat16 [512, 512], replicated
- edge_vec: float32 [4, 512], replicated
- node_w1: bfloat16 [1024, 512], replicated
- node_w2: bfloat16 [512, 512], replicated
- node_vec: float32 [4, 512], replicated
- post_w1: bfloat16 [512, 512], replicated
- post_w2: bfloat16 [512, 512], replicated
- post_vec: float32 [4, 512], replicated
- cot_mesh: bfloat16 [32768, 512], P(('batch', 'graph'))
- cot_grid: bfloat16 [65536, 512], P(('batch', 'graph'))
Outputs:
- output 1: bfloat16 [32768, 512], P(('batch', 'graph'))
- output 2: bfloat16 [65536, 512], P(('batch', 'graph'))
- output 3: float32 [65536, 186], P(('batch', 'graph'))
- output 4: float32 [1536, 512], P(('batch', 'graph'))
- output 5: float32 [512, 512], P(('batch', 'graph'))
All inputs are finite; a program needn't handle non-finite values.
Results may differ from a plain program's by a relative error of at most 0.00869367.
Values are sent between devices in bfloat16 or wider.
A program may use at most 1 GiB of HBM per device.

v0:
```python
import jax
import jax.numpy as jnp
from jax import lax
from jax.sharding import PartitionSpec as P

NORM_EPS = 1e-5


def mlp_forward(x_in, w_one, w_two, vec_rows):
    pre_one = jnp.dot(x_in, w_one, preferred_element_type=jnp.float32) + vec_rows[0]
    act_bf = jax.nn.silu(pre_one).astype(jnp.bfloat16)
    pre_two = jnp.dot(act_bf, w_two, preferred_element_type=jnp.float32) + vec_rows[1]
    centred = pre_two - jnp.mean(pre_two, axis=-1, keepdims=True)
    inv_std = lax.rsqrt(jnp.mean(centred * centred, axis=-1, keepdims=True) + NORM_EPS)
    normed = centred * inv_std
    return normed * vec_rows[2] + vec_rows[3], (pre_one, act_bf, normed, inv_std)


def mlp_backward(d_out, w_two, vec_rows, saved_acts):
    pre_one, act_bf, normed, inv_std = saved_acts
    d_norm = d_out * vec_rows[2]
    d_two = inv_std * (d_norm - jnp.mean(d_norm, axis=-1, keepdims=True)
                       - normed * jnp.mean(d_norm * normed, axis=-1, keepdims=True))
    g_two = d_two.astype(jnp.bfloat16)
    d_act = jnp.einsum('nj,kj->nk', g_two, w_two, preferred_element_type=jnp.float32)
    sig_pre = jax.nn.sigmoid(pre_one)
    d_one = d_act * sig_pre * (1.0 + pre_one * (1.0 - sig_pre))
    return d_one.astype(jnp.bfloat16), g_two


def solution(mesh):
    groups = mesh.shape['graph']
    row_spec = P(('batch', 'graph'), None)
    flat_spec = P(('batch', 'graph'))
    rep_spec = P(None, None)
    down_perm = [(src_dev, src_dev - 1) for src_dev in range(1, groups)]
    up_perm = [(src_dev, src_dev + 1) for src_dev in range(groups - 1)]

    def device_step(grid_in, mesh_in, edge_in, edge_src, edge_dst, edge_mask, grid_w1, grid_w2, grid_vec,
                    mesh_w1, mesh_w2, mesh_vec, embed_w1, embed_w2, embed_vec, edge_w1, edge_w2, edge_vec,
                    node_w1, node_w2, node_vec, post_w1, post_w2, post_vec, cot_mesh, cot_grid):
        band_rows = grid_in.shape[0]
        halo_rows = band_rows // 4
        latent = grid_w2.shape[1]
        mesh_rows = mesh_in.shape[0]
        band_index = lax.axis_index('graph')
        grid_y, grid_saved = mlp_forward(grid_in.astype(jnp.bfloat16), grid_w1, grid_w2, grid_vec)
        grid_h = grid_y.astype(jnp.bfloat16)
        from_above = lax.ppermute(grid_h[:halo_rows], 'graph', down_perm)
        from_below = lax.ppermute(grid_h[band_rows - halo_rows:], 'graph', up_perm)
        row_table = jnp.concatenate([from_below, grid_h, from_above], axis=0)
        local_src = edge_src - (band_index * band_rows - halo_rows)
        mesh_h = mlp_forward(mesh_in.astype(jnp.bfloat16), mesh_w1, mesh_w2, mesh_vec)[0].astype(jnp.bfloat16)
        edge_h = mlp_forward(edge_in.astype(jnp.bfloat16), embed_w1, embed_w2, embed_vec)[0].astype(jnp.bfloat16)
        edge_cat = jnp.concatenate([edge_h, row_table[local_src], mesh_h[edge_dst]], axis=1)
        edge_y, edge_saved = mlp_forward(edge_cat, edge_w1, edge_w2, edge_vec)
        keep_col = edge_mask.astype(jnp.float32)[:, None]
        message = keep_col * (edge_h.astype(jnp.float32) + edge_y)
        agg_sum = jax.ops.segment_sum(message, edge_dst, num_segments=mesh_rows).astype(jnp.bfloat16)
        node_y, node_saved = mlp_forward(jnp.concatenate([mesh_h, agg_sum], axis=1), node_w1, node_w2, node_vec)
        mesh_out = (mesh_h.astype(jnp.float32) + node_y).astype(jnp.bfloat16)
        post_y, post_saved = mlp_forward(grid_h, post_w1, post_w2, post_vec)
        grid_out = (grid_h.astype(jnp.float32) + post_y).astype(jnp.bfloat16)
        node_g1 = mlp_backward(cot_mesh.astype(jnp.float32), node_w2, node_vec, node_saved)[0]
        agg_grad = jnp.einsum('nj,kj->nk', node_g1, node_w1[latent:], preferred_element_type=jnp.float32)
        edge_g1, edge_g2 = mlp_backward(keep_col * agg_grad[edge_dst], edge_w2, edge_vec, edge_saved)
        w1_part = jnp.einsum('ek,ej->kj', edge_cat, edge_g1, preferred_element_type=jnp.float32)
        w2_part = jnp.einsum('ek,ej->kj', edge_saved[1], edge_g2, preferred_element_type=jnp.float32)
        src_grad = jnp.einsum('ej,kj->ek', edge_g1, edge_w1[latent:2 * latent], preferred_element_type=jnp.float32)
        table_grad = jax.ops.segment_sum(src_grad, local_src, num_segments=band_rows + 2 * halo_rows)
        tail_grad = lax.ppermute(table_grad[:halo_rows], 'graph', down_perm)
        head_grad = lax.ppermute(table_grad[band_rows + halo_rows:], 'graph', up_perm)
        edge_part = table_grad[halo_rows:band_rows + halo_rows] + jnp.concatenate(
            [head_grad, jnp.zeros((band_rows - 2 * halo_rows, latent), jnp.float32), tail_grad], axis=0)
        post_g1 = mlp_backward(cot_grid.astype(jnp.float32), post_w2, post_vec, post_saved)[0]
        grid_cot = cot_grid.astype(jnp.float32) + jnp.einsum('nj,kj->nk', post_g1, post_w1,
                                                             preferred_element_type=jnp.float32) + edge_part
        grid_g1 = mlp_backward(grid_cot, grid_w2, grid_vec, grid_saved)[0]
        grid_grad = jnp.einsum('nj,kj->nk', grid_g1, grid_w1, preferred_element_type=jnp.float32)
        w1_grad = lax.psum_scatter(w1_part, 'graph', scatter_dimension=0, tiled=True)
        w2_grad = lax.psum_scatter(w2_part, 'graph', scatter_dimension=0, tiled=True)
        return mesh_out, grid_out, grid_grad, w1_grad, w2_grad

    in_specs = (row_spec, row_spec, row_spec, flat_spec, flat_spec, flat_spec) + (rep_spec,) * 18 + (row_spec, row_spec)
    return jax.shard_map(device_step, mesh=mesh, in_specs=in_specs, out_specs=(row_spec,) * 5, check_vma=False)
```

profile of v0, /device:TPU:1, one launch (start us, length us, event | category | flops | bytes accessed | tf_op | source)
XLA Modules:
  0.0 1000.0 jit_solution(17869728577826888309)
XLA Ops:
  20.1 13.4 %add_reduce_fusion.1 = (f32[8192]{0:T(1024)S(1)}, f32[8192,512]{1,0:T(8,128)}) fusion(f32[512]{0:T(512)S(1)} %bitcast.57, bf16[512,512]{1,0:T(8,128)(2,1)} %param.39, bf16[4,512]{1,0:T(4,128)(2,1)} %param.38, f32[512]{0:T(512)S(1)} %bitcast.89, f32[8192,4]{0,1:T(4,128)} %param.28), kind=kOutput, calls=%fused_computation.24 | convolution fusion | flops 4362100736 | bytes 17473536 | tf_op jit(solution)/shard_map/dot_general | solution.py:12
  33.5 7.7 multiply_reduce_fusion.2
  43.7 33.6 %gather_fusion.1 = bf16[8192,512]{1,0:T(8,128)(2,1)} fusion(bf16[256,512]{1,0:T(8,128)(2,1)S(1)} %add_convert_fusion.4, s32[8192]{0:T(1024)S(1)} %fusion.95), kind=kCustom, calls=%fused_computation.1 | custom fusion | bytes 16809984 | tf_op jit(solution)/shard_map/gather | solution.py:55
  77.7 10.5 %add_convert_fusion = bf16[8192,512]{1,0:T(8,128)(2,1)} fusion(f32[8192,512]{1,0:T(8,128)} %get-tuple-element.46, f32[512]{0:T(512)S(1)} %bitcast.70, f32[512]{0:T(512)S(1)} %bitcast.72, f32[8192]{0:T(1024)S(1)} %add_rsqrt_fusion.1, f32[8192]{0:T(1024)S(1)} %broadcast_multiply_fusion.3, f32[512]{0:T(512)S(1)} %bitcast.59), kind=kLoop, calls=%fused_computation.19 | loop fusion | flops 25165824 | bytes 25237504 | tf_op jit(solution)/shard_map/convert_element_type | solution.py:54
  90.3 33.6 %gather_fusion = bf16[8192,512]{1,0:T(8,128)(2,1)} fusion(bf16[768,512]{1,0:T(8,128)(2,1)S(1)} %pad_maximum_fusion.3, s32[8192]{0:T(1024)S(1)} %get-tuple-element.13), kind=kCustom, calls=%fused_computation | custom fusion | bytes 16809984 | tf_op jit(solution)/shard_map/gather | solution.py:55
  123.9 24.8 %multiply_convert_fusion.2 = (bf16[8192,512]{1,0:T(8,128)(2,1)}, f32[8192,512]{1,0:T(8,128)}) fusion(f32[512]{0:T(512)S(1)} %bitcast.83, bf16[1536,512]{1,0:T(8,128)(2,1)} %param.41, bf16[8192,512]{1,0:T(8,128)(2,1)} %gather_fusion.1, bf16[8192,512]{1,0:T(8,128)(2,1)} %gather_fusion, bf16[8192,512]{1,0:T(8,128)(2,1)} %add_convert_fusion), kind=kOutput, calls=%fused_computation.16 | convolution fusion | flops 12985565184 | bytes 51906560 | tf_op jit(solution)/shard_map/dot_general | solution.py:10
  148.7 7.2 add_reduce_fusion
  155.9 5.7 copy-done.1
  165.5 61.0 %scatter_custom_fusion = f32[256,512]{1,0:T(8,128)S(1)} fusion(s32[8192]{0:T(1024)S(1)} %copy-done.41, f32[8192,512]{1,0:T(8,128)} %copy-done.1, f32[512]{0:T(512)S(1)} %bitcast.80, f32[512]{0:T(512)S(1)} %bitcast.54, f32[8192]{0:T(1024)S(1)} %add_rsqrt_fusion, f32[8192]{0:T(1024)S(1)} %broadcast_multiply_fusion.2, f32[512]{0:T(512)S(1)} %bitcast.51, ...), kind=kCustom, calls=%fused_computation.10 | custom fusion | flops 62914560 | bytes 34254852 | tf_op jit(solution)/shard_map/scatter-add | solution.py:59
  233.2 32.7 %gather_fusion.2 = f32[8192,512]{1,0:T(8,128)} fusion(f32[256,512]{1,0:T(8,128)S(1)} %fusion.26, s32[8192]{0:T(1024)S(1)} %fusion.95), kind=kCustom, calls=%fused_computation.2 | custom fusion | bytes 33587200 | tf_op jit(solution)/shard_map/gather | solution.py:66
  265.8 13.5 %fusion.7 = (f32[8192]{0:T(1024)S(1)}, f32[8192]{0:T(1024)S(1)}) fusion(f32[8192,512]{1,0:T(8,128)} %gather_fusion.2, f32[512]{0:T(512)S(1)} %bitcast.55, f32[8192]{0:T(1024)S(1)} %convert_element_type.92, f32[8192]{0:T(1024)S(1)} %add_rsqrt_fusion, f32[8192]{0:T(1024)S(1)} %broadcast_multiply_fusion.2, f32[8192,512]{1,0:T(8,128)} %copy-done.1, ...), kind=kLoop, calls=%fused_computation.25 | loop fusion | flops 33538048 | bytes 33722368 | tf_op jit(solution)/shard_map/reduce_sum | solution.py:22
  281.2 11.9 %multiply_convert_fusion.1 = bf16[8192,512]{1,0:T(8,128)(2,1)} fusion(f32[8192,512]{1,0:T(8,128)S(1)} %copy-done.2, f32[8192,512]{1,0:T(8,128)} %copy-done.1, f32[8192]{0:T(1024)S(1)} %broadcast_multiply_fusion, f32[8192]{0:T(1024)S(1)} %broadcast_multiply_fusion.1, f32[512]{0:T(512)S(1)} %bitcast.56, f32[8192]{0:T(1024)S(1)} %add_rsqrt_fusion, ...), kind=kLoop, calls=%fused_computation.7 | loop fusion | flops 41943040 | bytes 42110976 | tf_op jit(solution)/shard_map/convert_element_type | solution.py:24
  293.1 12.8 %multiply_convert_fusion = bf16[8192,512]{1,0:T(8,128)(2,1)S(1)} fusion(f32[8192,512]{1,0:T(8,128)} %get-tuple-element.52, bf16[8192,512]{1,0:T(8,128)(2,1)} %multiply_convert_fusion.1, bf16[512,512]{1,0:T(8,128)(2,1)S(1)} %copy-done, f32[512]{0:T(512)S(1)} %bitcast.84), kind=kOutput, calls=%fused_computation.6 | convolution fusion | flops 4336910336 | bytes 34080768 | tf_op jit(solution)/shard_map/nj,kj->nk/dot_general | solution.py:25
  309.2 18.6 %fusion.8 = f32[1536,512]{1,0:T(8,128)} fusion(bf16[8192,512]{1,0:T(8,128)(2,1)S(1)} %multiply_convert_fusion, bf16[8192,512]{1,0:T(8,128)(2,1)} %gather_fusion.1, bf16[8192,512]{1,0:T(8,128)(2,1)} %gather_fusion, bf16[8192,512]{1,0:T(8,128)(2,1)} %add_convert_fusion), kind=kOutput, calls=%fused_computation.26 | convolution fusion | flops 12960399360 | bytes 36700160 | tf_op jit(solution)/shard_map/ek,ej->kj/dot_general | solution.py:67
  327.8 336.4 %fusion = f32[16,512]{1,0:T(8,128)S(1)} fusion(f32[1536,512]{1,0:T(8,128)} %fusion.8), kind=kCustom, calls=%all-reduce-scatter | all-reduce-scatter fusion | flops 1048577 | bytes 3178496
  676.3 20.4 %collective-permute-start.18 = (f32[16,512]{1,0:T(8,128)S(1)}, f32[16,512]{1,0:T(8,128)S(1)}, u32[]{:S(2)}, u32[]{:S(2)}) collective-permute-start(f32[16,512]{1,0:T(8,128)S(1)} %fusion), channel_id=1, source_target_pairs={{0,15},{1,16},{2,17},{3,18},{4,19},{5,20},{6,21},{7,22},{8,23},{9,... | collective-permute-start | bytes 98312
  696.7 10.5 %collective-permute-start.19 = (f32[16,512]{1,0:T(8,128)S(1)}, f32[16,512]{1,0:T(8,128)S(1)}, u32[]{:S(2)}, u32[]{:S(2)}) collective-permute-start(f32[16,512]{1,0:T(8,128)S(1)} %fusion), channel_id=1, source_target_pairs={{0,16},{1,17},{2,18},{3,19},{4,20},{5,21},{6,22},{7,23},{8,24},{9,... | collective-permute-start | bytes 98312
  709.8 5.4 collective-permute-start.21
  739.4 13.7 %fusion.51 = f32[8192,512]{1,0:T(8,128)} fusion(bf16[8192,512]{1,0:T(8,128)(2,1)} %copy-done.3, bf16[1536,512]{1,0:T(8,128)(2,1)} %param.41), kind=kOutput, calls=%fused_computation.92 | convolution fusion | flops 4294967296 | bytes 25690112 | tf_op jit(solution)/shard_map/ej,kj->ek/dot_general | solution.py:69
  753.3 50.4 %scatter_custom_fusion.1 = f32[768,512]{1,0:T(8,128)} fusion(s32[8192]{0:T(1024)} %get-tuple-element.14, f32[8192,512]{1,0:T(8,128)} %fusion.51, f32[]{:T(128)} %constant.51.clone.1), kind=kCustom, calls=%fused_computation.84 | custom fusion | flops 4194304 | bytes 1573376 | tf_op jit(solution)/shard_map/scatter-add | solution.py:70
  815.4 5.1 collective-permute-start.7
  832.8 11.3 %fusion.128 = f32[512,512]{1,0:T(8,128)} fusion(bf16[8192,512]{1,0:T(8,128)(2,1)} %get-tuple-element.51, bf16[8192,512]{1,0:T(8,128)(2,1)} %multiply_convert_fusion.1), kind=kOutput, calls=%fused_computation.185 | convolution fusion | flops 4294967296 | bytes 17825792 | tf_op jit(solution)/shard_map/ek,ej->kj/dot_general | solution.py:68
  844.1 45.9 %concatenate.16 = f32[524,512]{1,0:T(8,128)} concatenate(f32[12,512]{1,0:T(8,128)S(1)} %collective-permute-done.35, f32[16,512]{1,0:T(8,128)} %copy-done.33, f32[16,512]{1,0:T(8,128)} %copy-done.32, f32[16,512]{1,0:T(8,128)} %copy-done.31, f32[16,512]{1,0:T(8,128)} %copy-done.30, f32[16,512]{1,0:T(8,128)} %copy-done.29, f32[16,512]{1,0:T(8,128)} %copy-done.28, ...), dimensions={0} | concatenate | bytes 2146304
  900.7 90.7 %all-reduce.5.cloned.1.call-done = f32[512,512]{1,0:T(8,128)} async-done(((f32[512,512]{1,0:T(8,128)}), f32[512,512]{1,0:T(8,128)}) %all-reduce.5.cloned.1.call-update) | async-done | bytes 1048592
  (243 shorter events, 107.4 us)
Async XLA Ops:
  7.2 984.2 %all-reduce.5.cloned.1.call-start = ((), (), s32[]{:S(2)}) async-start(), calls=%async_computation | async-start | bytes 2097152
  12.7 77.5 %collective-permute-start = (bf16[128,512]{1,0:T(8,128)(2,1)S(1)}, bf16[128,512]{1,0:T(8,128)(2,1)S(1)}, u32[]{:S(2)}, u32[]{:S(2)}) collective-permute-start(bf16[128,512]{1,0:T(8,128)(2,1)S(1)} %get-tuple-element.19), channel_id=1, source_target_pairs={{0,1},{1,2},{2,3},{3,4},{4,5},{5,6},{6,7},{7,8},{8,9},{9,10},{10,1... | collective-permute-start | bytes 393224 | tf_op jit(solution)/shard_map/ppermute | solution.py:50
  17.2 73.0 %collective-permute-start.1 = (bf16[128,512]{1,0:T(8,128)(2,1)S(1)}, bf16[128,512]{1,0:T(8,128)(2,1)S(1)}, u32[]{:S(2)}, u32[]{:S(2)}) collective-permute-start(bf16[128,512]{1,0:T(8,128)(2,1)S(1)} %get-tuple-element.20), channel_id=1, source_target_pairs={{1,0},{2,1},{3,2},{4,3},{5,4},{6,5},{7,6},{8,7},{9,8},{10,9},{11,1... | collective-permute-start | bytes 393224 | tf_op jit(solution)/shard_map/ppermute | solution.py:49
  671.0 25.7 %collective-permute-start.14 = (f32[16,512]{1,0:T(8,128)S(1)}, f32[16,512]{1,0:T(8,128)S(1)}, u32[]{:S(2)}, u32[]{:S(2)}) collective-permute-start(f32[16,512]{1,0:T(8,128)S(1)} %fusion), channel_id=1, source_target_pairs={{0,11},{1,12},{2,13},{3,14},{4,15},{5,16},{6,17},{7,18},{8,19},{9,... | collective-permute-start | bytes 98312
  672.3 34.9 %collective-permute-start.15 = (f32[16,512]{1,0:T(8,128)S(1)}, f32[16,512]{1,0:T(8,128)S(1)}, u32[]{:S(2)}, u32[]{:S(2)}) collective-permute-start(f32[16,512]{1,0:T(8,128)S(1)} %fusion), channel_id=1, source_target_pairs={{0,12},{1,13},{2,14},{3,15},{4,16},{5,17},{6,18},{7,19},{8,20},{9,... | collective-permute-start | bytes 98312
  673.7 36.2 %collective-permute-start.16 = (f32[16,512]{1,0:T(8,128)S(1)}, f32[16,512]{1,0:T(8,128)S(1)}, u32[]{:S(2)}, u32[]{:S(2)}) collective-permute-start(f32[16,512]{1,0:T(8,128)S(1)} %fusion), channel_id=1, source_target_pairs={{0,13},{1,14},{2,15},{3,16},{4,17},{5,18},{6,19},{7,20},{8,21},{9,... | collective-permute-start | bytes 98312
  675.0 40.3 %collective-permute-start.17 = (f32[16,512]{1,0:T(8,128)S(1)}, f32[16,512]{1,0:T(8,128)S(1)}, u32[]{:S(2)}, u32[]{:S(2)}) collective-permute-start(f32[16,512]{1,0:T(8,128)S(1)} %fusion), channel_id=1, source_target_pairs={{0,14},{1,15},{2,16},{3,17},{4,18},{5,19},{6,20},{7,21},{8,22},{9,... | collective-permute-start | bytes 98312
  676.3 44.9 %collective-permute-start.18 = (f32[16,512]{1,0:T(8,128)S(1)}, f32[16,512]{1,0:T(8,128)S(1)}, u32[]{:S(2)}, u32[]{:S(2)}) collective-permute-start(f32[16,512]{1,0:T(8,128)S(1)} %fusion), channel_id=1, source_target_pairs={{0,15},{1,16},{2,17},{3,18},{4,19},{5,20},{6,21},{7,22},{8,23},{9,... | collective-permute-start | bytes 98312
  696.7 26.1 %collective-permute-start.19 = (f32[16,512]{1,0:T(8,128)S(1)}, f32[16,512]{1,0:T(8,128)S(1)}, u32[]{:S(2)}, u32[]{:S(2)}) collective-permute-start(f32[16,512]{1,0:T(8,128)S(1)} %fusion), channel_id=1, source_target_pairs={{0,16},{1,17},{2,18},{3,19},{4,20},{5,21},{6,22},{7,23},{8,24},{9,... | collective-permute-start | bytes 98312
  707.3 17.2 %collective-permute-start.20 = (f32[16,512]{1,0:T(8,128)S(1)}, f32[16,512]{1,0:T(8,128)S(1)}, u32[]{:S(2)}, u32[]{:S(2)}) collective-permute-start(f32[16,512]{1,0:T(8,128)S(1)} %fusion), channel_id=1, source_target_pairs={{0,17},{1,18},{2,19},{3,20},{4,21},{5,22},{6,23},{7,24},{8,25},{9,... | collective-permute-start | bytes 98312
  709.8 16.9 %collective-permute-start.21 = (f32[16,512]{1,0:T(8,128)S(1)}, f32[16,512]{1,0:T(8,128)S(1)}, u32[]{:S(2)}, u32[]{:S(2)}) collective-permute-start(f32[16,512]{1,0:T(8,128)S(1)} %fusion), channel_id=1, source_target_pairs={{0,18},{1,19},{2,20},{3,21},{4,22},{5,23},{6,24},{7,25},{8,26},{9,... | collective-permute-start | bytes 98312
  730.3 73.3 %collective-permute-start.28 = (f32[16,512]{1,0:T(8,128)S(1)}, f32[16,512]{1,0:T(8,128)S(1)}, u32[]{:S(2)}, u32[]{:S(2)}) collective-permute-start(f32[16,512]{1,0:T(8,128)S(1)} %fusion), channel_id=1, source_target_pairs={{0,25},{1,26},{2,27},{3,28},{4,29},{5,30},{6,31},{7,32},{8,33},{9,... | collective-permute-start | bytes 98312
  731.9 73.1 %collective-permute-start.29 = (f32[16,512]{1,0:T(8,128)S(1)}, f32[16,512]{1,0:T(8,128)S(1)}, u32[]{:S(2)}, u32[]{:S(2)}) collective-permute-start(f32[16,512]{1,0:T(8,128)S(1)} %fusion), channel_id=1, source_target_pairs={{0,26},{1,27},{2,28},{3,29},{4,30},{5,31},{6,32},{7,33},{8,34},{9,... | collective-permute-start | bytes 98312
  733.6 72.7 %collective-permute-start.30 = (f32[16,512]{1,0:T(8,128)S(1)}, f32[16,512]{1,0:T(8,128)S(1)}, u32[]{:S(2)}, u32[]{:S(2)}) collective-permute-start(f32[16,512]{1,0:T(8,128)S(1)} %fusion), channel_id=1, source_target_pairs={{0,27},{1,28},{2,29},{3,30},{4,31},{5,32},{6,33},{7,34},{8,35},{9,... | collective-permute-start | bytes 98312
  736.4 72.1 %collective-permute-start.31 = (f32[16,512]{1,0:T(8,128)S(1)}, f32[16,512]{1,0:T(8,128)S(1)}, u32[]{:S(2)}, u32[]{:S(2)}) collective-permute-start(f32[16,512]{1,0:T(8,128)S(1)} %fusion), channel_id=1, source_target_pairs={{0,28},{1,29},{2,30},{3,31},{4,32},{5,33},{6,34},{7,35},{8,36},{9,... | collective-permute-start | bytes 98312
  738.1 72.7 %collective-permute-start.32 = (f32[16,512]{1,0:T(8,128)S(1)}, f32[16,512]{1,0:T(8,128)S(1)}, u32[]{:S(2)}, u32[]{:S(2)}) collective-permute-start(f32[16,512]{1,0:T(8,128)S(1)} %fusion), channel_id=1, source_target_pairs={{0,29},{1,30},{2,31},{3,32},{4,33},{5,34},{6,35},{7,36},{8,37},{9,... | collective-permute-start | bytes 98312
  806.3 18.5 %collective-permute-start.4 = (f32[16,512]{1,0:T(8,128)S(1)}, f32[16,512]{1,0:T(8,128)S(1)}, u32[]{:S(2)}, u32[]{:S(2)}) collective-permute-start(f32[16,512]{1,0:T(8,128)S(1)} %fusion), channel_id=1, source_target_pairs={{0,1},{1,2},{2,3},{3,4},{4,5},{5,6},{6,7},{7,8},{8,9},{9,10},{10,1... | collective-permute-start | bytes 98312
  808.6 18.2 %collective-permute-start.5 = (f32[16,512]{1,0:T(8,128)S(1)}, f32[16,512]{1,0:T(8,128)S(1)}, u32[]{:S(2)}, u32[]{:S(2)}) collective-permute-start(f32[16,512]{1,0:T(8,128)S(1)} %fusion), channel_id=1, source_target_pairs={{0,2},{1,3},{2,4},{3,5},{4,6},{5,7},{6,8},{7,9},{8,10},{9,11},{10,... | collective-permute-start | bytes 98312
  810.8 18.1 %collective-permute-start.6 = (f32[16,512]{1,0:T(8,128)S(1)}, f32[16,512]{1,0:T(8,128)S(1)}, u32[]{:S(2)}, u32[]{:S(2)}) collective-permute-start(f32[16,512]{1,0:T(8,128)S(1)} %fusion), channel_id=1, source_target_pairs={{0,3},{1,4},{2,5},{3,6},{4,7},{5,8},{6,9},{7,10},{8,11},{9,12},{10... | collective-permute-start | bytes 98312
  815.4 28.6 %collective-permute-start.7 = (f32[16,512]{1,0:T(8,128)S(1)}, f32[16,512]{1,0:T(8,128)}, u32[]{:S(2)}, u32[]{:S(2)}) collective-permute-start(f32[16,512]{1,0:T(8,128)S(1)} %fusion), channel_id=1, source_target_pairs={{0,4},{1,5},{2,6},{3,7},{4,8},{5,9},{6,10},{7,11},{8,12},{9,13},{1... | collective-permute-start | bytes 98312
  820.5 23.5 %collective-permute-start.8 = (f32[16,512]{1,0:T(8,128)S(1)}, f32[16,512]{1,0:T(8,128)}, u32[]{:S(2)}, u32[]{:S(2)}) collective-permute-start(f32[16,512]{1,0:T(8,128)S(1)} %fusion), channel_id=1, source_target_pairs={{0,5},{1,6},{2,7},{3,8},{4,9},{5,10},{6,11},{7,12},{8,13},{9,14},{... | collective-permute-start | bytes 98312
  824.9 19.2 %collective-permute-start.9 = (f32[16,512]{1,0:T(8,128)S(1)}, f32[16,512]{1,0:T(8,128)}, u32[]{:S(2)}, u32[]{:S(2)}) collective-permute-start(f32[16,512]{1,0:T(8,128)S(1)} %fusion), channel_id=1, source_target_pairs={{0,6},{1,7},{2,8},{3,9},{4,10},{5,11},{6,12},{7,13},{8,14},{9,15},... | collective-permute-start | bytes 98312
  826.7 64.7 %collective-permute-start.2 = (f32[128,512]{1,0:T(8,128)S(1)}, f32[128,512]{1,0:T(8,128)}, u32[]{:S(2)}, u32[]{:S(2)}) collective-permute-start(f32[128,512]{1,0:T(8,128)S(1)} %get-tuple-element.15), channel_id=1, source_target_pairs={{0,1},{1,2},{2,3},{3,4},{4,5},{5,6},{6,7},{7,8},{8,9},{9,10},{10,1... | collective-permute-start | bytes 786440 | tf_op jit(solution)/shard_map/ppermute | solution.py:72
  829.6 61.8 %collective-permute-start.3 = (f32[128,512]{1,0:T(8,128)S(1)}, f32[128,512]{1,0:T(8,128)}, u32[]{:S(2)}, u32[]{:S(2)}) collective-permute-start(f32[128,512]{1,0:T(8,128)S(1)} %get-tuple-element.16), channel_id=1, source_target_pairs={{1,0},{2,1},{3,2},{4,3},{5,4},{6,5},{7,6},{8,7},{9,8},{10,9},{11,1... | collective-permute-start | bytes 786440 | tf_op jit(solution)/shard_map/ppermute | solution.py:71
  (73 other events, 4726.0 us)
Sparse Core Ops, SparseCore 0:
  844.2 147.1 all-reduce.4
where the time goes:
time: 1010 us; the launch traced here: 1000 us
  blocking collectives  336 us (33%)
  local copies, waits for them, and re-layouts  165 us (16%)
  other arithmetic  165 us (16%)
  matrix products  121 us (12%)
  starting transfers between devices  105 us (10%)
  waiting for transfers between devices  90.8 us (9%)
  between operations  16 us (2%)
    unnamed x1, blocking collectives  336 us
    unnamed x33, starting transfers between devices  93.7 us
    unnamed x34, waiting for transfers between devices  90.8 us
    unnamed x124, local copies, waits for them, and re-layouts  61 us
    scatter-add x1, other arithmetic, device_step(): jax.ops.segment_sum(message, edge_dst, num_segments=mesh_rows)  61 us
    scatter-add x1, other arithmetic, device_step(): jax.ops.segment_sum(src_grad, local_src, num_segments=band_rows + 2 * hal...  50.4 us
    gather x1, local copies, waits for them, and re-layouts, device_step(): row_table[local_src]  33.6 us
    gather x1, local copies, waits for them, and re-layouts, device_step(): mesh_h[edge_dst]  33.6 us
  transfers between devices with their start and end apart: 37, of which 1 were waited for; matrix products, arithmetic and copies ran while one was open for 21% of the time, Pallas kernels for 0%

commit v1 on v0

v1 whole, which is shorter than its diff:
```python
import functools

import jax
import jax.numpy as jnp
from jax import lax
from jax.experimental import pallas as pl
from jax.experimental.pallas import tpu as pltpu
from jax.sharding import PartitionSpec as P

NORM_EPS = 1e-5
BF = jnp.bfloat16
F32 = jnp.float32
VMEM = pltpu.VMEM
CHUNK = 512


def mlp_forward(x_in, w_one, w_two, vec_rows):
    pre_one = jnp.dot(x_in, w_one, preferred_element_type=F32) + vec_rows[0]
    act_bf = jax.nn.silu(pre_one).astype(BF)
    pre_two = jnp.dot(act_bf, w_two, preferred_element_type=F32) + vec_rows[1]
    centred = pre_two - jnp.mean(pre_two, axis=-1, keepdims=True)
    inv_std = lax.rsqrt(jnp.mean(centred * centred, axis=-1, keepdims=True) + NORM_EPS)
    normed = centred * inv_std
    return normed * vec_rows[2] + vec_rows[3], (pre_one, act_bf, normed, inv_std)


def mlp_backward(d_out, w_two, vec_rows, saved_acts):
    pre_one, act_bf, normed, inv_std = saved_acts
    d_norm = d_out * vec_rows[2]
    d_two = inv_std * (d_norm - jnp.mean(d_norm, axis=-1, keepdims=True)
                       - normed * jnp.mean(d_norm * normed, axis=-1, keepdims=True))
    g_two = d_two.astype(BF)
    d_act = jnp.einsum('nj,kj->nk', g_two, w_two, preferred_element_type=F32)
    sig_pre = jax.nn.sigmoid(pre_one)
    d_one = d_act * sig_pre * (1.0 + pre_one * (1.0 - sig_pre))
    return d_one.astype(BF), g_two


def dot_nn(a, b):
    return jnp.dot(a, b, preferred_element_type=F32)


def dot_nt(a, b):
    return lax.dot_general(a, b, (((1,), (1,)), ((), ())), preferred_element_type=F32)


def dot_tn(a, b):
    return lax.dot_general(a, b, (((0,), (0,)), ((), ())), preferred_element_type=F32)


def split3(x):
    hi = x.astype(BF)
    rest = x - hi.astype(F32)
    mid = rest.astype(BF)
    low = (rest - mid.astype(F32)).astype(BF)
    return hi, mid, low


def silu_bf(p):
    h = 0.5 * p
    return (h + h * jnp.tanh(h)).astype(BF)


def norm_cols(q):
    centred = q - jnp.mean(q, axis=0, keepdims=True)
    inv = lax.rsqrt(jnp.mean(centred * centred, axis=0, keepdims=True) + NORM_EPS)
    return centred * inv, inv


def col(vec_ref, k):
    return vec_ref[:, k:k + 1]


def grad_first(d_act, p):
    t = jnp.tanh(0.5 * p)
    s = 0.5 + 0.5 * t
    return (d_act * (s * (1.0 + p * (1.0 - s)))).astype(BF)


def one_hot(rows, idx):
    return (lax.broadcasted_iota(jnp.int32, (rows, idx.shape[1]), 0) == idx).astype(F32).astype(BF)


def edge_kernel(x_ref, src_ref, dst_ref, dstm_ref, table_ref, hm_ref, cotm_ref, wa_ref, em_w2t_ref, em_vec_ref,
                w1t_ref, w2t_ref, w2_ref, ed_vec_ref, nw1t_ref, nw2t_ref, nd_vec_ref,
                mesh_out_ref, w1g_ref, w2g_ref, tgrad_ref,
                pre_s, norm_s, he_s, inv_s, wl_s, bt_s, agg_s):
    lat = w2_ref.shape[0]
    nt = table_ref.shape[1]
    nm = hm_ref.shape[1]
    steps = pre_s.shape[0]
    ch = pre_s.shape[2]

    wl_s[:, 0:2 * lat] = w1t_ref[:, 0:2 * lat]
    pm = dot_nn(w1t_ref[:, 2 * lat:3 * lat], hm_ref[...]) + col(ed_vec_ref, 0)
    for k, part in enumerate(split3(pm)):
        wl_s[:, 2 * lat + k * nm:2 * lat + (k + 1) * nm] = part
    agg_s[...] = jnp.zeros_like(agg_s)

    def fwd(i, carry):
        sl = pl.ds(pl.multiple_of(i * ch, ch), ch)
        pe = dot_nn(wa_ref[...], x_ref[:, sl])
        ne, _ = norm_cols(dot_nn(em_w2t_ref[...], silu_bf(pe)) + col(em_vec_ref, 1))
        he = (ne * col(em_vec_ref, 2) + col(em_vec_ref, 3)).astype(BF)
        he_s[i] = he
        gath = dot_nn(table_ref[...], one_hot(nt, src_ref[:, sl])).astype(BF)
        ohd = one_hot(nm, dst_ref[:, sl])
        p = dot_nn(wl_s[...], jnp.concatenate([he, gath, ohd, ohd, ohd], axis=0))
        pre_s[i] = p
        n, inv = norm_cols(dot_nn(w2t_ref[...], silu_bf(p)) + col(ed_vec_ref, 1))
        norm_s[i] = n
        inv_s[i] = inv
        msg = he.astype(F32) + (n * col(ed_vec_ref, 2) + col(ed_vec_ref, 3))
        ohm = one_hot(nm, dstm_ref[:, sl])
        agg_s[...] += dot_nt(jnp.concatenate(split3(msg), axis=1), jnp.concatenate([ohm, ohm, ohm], axis=1))
        return carry

    lax.fori_loop(0, steps, fwd, 0)

    hm = hm_ref[...]
    np_ = dot_nn(nw1t_ref[...], jnp.concatenate([hm, agg_s[...].astype(BF)], axis=0)) + col(nd_vec_ref, 0)
    nn_, ninv = norm_cols(dot_nn(nw2t_ref[...], silu_bf(np_)) + col(nd_vec_ref, 1))
    mesh_out_ref[...] = (hm.astype(F32) + (nn_ * col(nd_vec_ref, 2) + col(nd_vec_ref, 3))).astype(BF)
    dn = cotm_ref[...].astype(F32) * col(nd_vec_ref, 2)
    d2 = ninv * (dn - jnp.mean(dn, axis=0, keepdims=True) - nn_ * jnp.mean(dn * nn_, axis=0, keepdims=True))
    ng1 = grad_first(dot_tn(nw2t_ref[...], d2.astype(BF)), np_)
    ag = dot_tn(nw1t_ref[:, lat:2 * lat], ng1) * col(ed_vec_ref, 2)
    ag = ag - jnp.mean(ag, axis=0, keepdims=True)
    for k, part in enumerate(split3(ag)):
        bt_s[:, k * nm:(k + 1) * nm] = part

    w1g_ref[...] = jnp.zeros_like(w1g_ref)
    w2g_ref[...] = jnp.zeros_like(w2g_ref)

    def bwd(i, carry):
        sl = pl.ds(pl.multiple_of(i * ch, ch), ch)
        ohm = one_hot(nm, dstm_ref[:, sl])
        bg = dot_nn(bt_s[...], jnp.concatenate([ohm, ohm, ohm], axis=0))
        n = norm_s[i]
        g2 = (inv_s[i] * (bg - n * jnp.mean(bg * n, axis=0, keepdims=True))).astype(BF)
        p = pre_s[i]
        w2g_ref[...] += dot_nt(silu_bf(p), g2)
        g1 = grad_first(dot_nn(w2_ref[...], g2), p)
        w1g_ref[...] += dot_nt(jnp.concatenate([he_s[i], one_hot(nt, src_ref[:, sl]), ohm], axis=0), g1)
        return carry

    lax.fori_loop(0, steps, bwd, 0)

    sp = split3(w1g_ref[lat:lat + nt, :])
    tp = split3(w1g_ref[lat + nt:lat + nt + nm, :])
    table = table_ref[...]
    w1g_ref[lat:2 * lat, :] = dot_nn(jnp.concatenate([table, table, table], axis=1), jnp.concatenate(sp, axis=0))
    w1g_ref[2 * lat:3 * lat, :] = dot_nn(jnp.concatenate([hm, hm, hm], axis=1),
                                         jnp.concatenate(tp, axis=0))
    wb = w1t_ref[:, lat:2 * lat].T
    tgrad_ref[...] = dot_nt(jnp.concatenate([wb, wb, wb], axis=1), jnp.concatenate(sp, axis=1))


def edge_call(x_aug, src, dst, dstm, table, hm, cotm, wa, em_w2t, em_vec, w1t, w2t, w2, ed_vec,
              nw1t, nw2t, nd_vec):
    lat, nt, nm, edges = w2.shape[0], table.shape[1], hm.shape[1], src.shape[1]
    steps = edges // CHUNK
    out_shape = (jax.ShapeDtypeStruct((lat, nm), BF), jax.ShapeDtypeStruct((3 * lat, lat), F32),
                 jax.ShapeDtypeStruct((lat, lat), F32), jax.ShapeDtypeStruct((lat, nt), F32))
    return pl.pallas_call(
        edge_kernel,
        out_shape=out_shape,
        in_specs=[pl.BlockSpec(memory_space=VMEM)] * 17,
        out_specs=(pl.BlockSpec(memory_space=VMEM),) * 4,
        scratch_shapes=[VMEM((steps, lat, CHUNK), F32), VMEM((steps, lat, CHUNK), F32), VMEM((steps, lat, CHUNK), BF),
                        VMEM((steps, 1, CHUNK), F32), VMEM((lat, 2 * lat + 3 * nm), BF), VMEM((lat, 3 * nm), BF),
                        VMEM((lat, nm), F32)],
        compiler_params=pltpu.CompilerParams(vmem_limit_bytes=67043328),
        name='edge_pass',
    )(x_aug, src, dst, dstm, table, hm, cotm, wa, em_w2t, em_vec, w1t, w2t, w2, ed_vec,
      nw1t, nw2t, nd_vec)


def scatter_kernel(w1_ref, w2_ref, o1_ref, o2_ref,
                   r0a, r0b, r0c, a0, b0, c0, ra1, rb1, rc1, a1, b1, c1, ra2, rb2, rc2, a2, b2, c2, ra3, rb3, rc3,
                   f1, f2, rf1, rf2, send0, recv0, sends, recvs, send4, recv4):
    me = lax.axis_index('graph')
    core = lax.rem(me, 2)
    chip = me // 2
    px, py, pz = lax.rem(chip, 4), lax.rem(chip // 4, 4), chip // 16

    def dev(z, y, x, k):
        return {'graph': ((z * 4 + y) * 4 + x) * 2 + k}

    def turn(v, d):
        return lax.rem(v + d, 4)

    partner = dev(pz, py, px, 1 - core)
    peers = {'x': [dev(pz, py, turn(px, d), core) for d in (1, 2, 3)],
             'y': [dev(pz, turn(py, d), px, core) for d in (1, 2, 3)],
             'z': [dev(turn(pz, d), py, px, core) for d in (1, 2, 3)]}
    pos = {'x': px, 'y': py, 'z': pz}
    barrier = pltpu.get_barrier_semaphore()
    for peer in [partner] + peers['x'] + peers['y'] + peers['z']:
        pl.semaphore_signal(barrier, inc=1, device_id=peer, device_id_type=pl.DeviceIdType.MESH)
    pl.semaphore_wait(barrier, 10)

    half = w1_ref.shape[-1] // 2
    mine = pl.multiple_of(core * half, half)
    his = pl.multiple_of((1 - core) * half, half)
    q = half // 2

    def copy(src, dst, ssem, rsem, peer):
        c = pltpu.make_async_remote_copy(src_ref=src, dst_ref=dst, send_sem=ssem, recv_sem=rsem, device_id=peer,
                                         device_id_type=pl.DeviceIdType.MESH)
        c.start()
        return c

    first = [copy(w1_ref.at[:, :, :, :, pl.ds(his, q)], r0a, send0.at[0], recv0.at[0], partner),
             copy(w1_ref.at[:, :, :, :, pl.ds(pl.multiple_of(his + q, q), q)], r0b, send0.at[1], recv0.at[1], partner),
             copy(w2_ref.at[:, :, :, :, pl.ds(his, half)], r0c, send0.at[2], recv0.at[2], partner)]

    def pick(ref, axis_at, v):
        if axis_at == 0:
            return ref.at[v]
        if axis_at == 1:
            return ref.at[:, v]
        return ref.at[:, :, v]

    plans = {'a': [('x', 2), ('y', 1), ('z', 0)], 'b': [('y', 1), ('z', 0), ('x', 0)],
             'c': [('z', 0), ('x', 1), ('y', 0)]}
    accs = {'a': [a0, a1, a2, f1.at[:, pl.ds(0, q)]], 'b': [b0, b1, b2, f1.at[:, pl.ds(q, q)]], 'c': [c0, c1, c2, f2]}
    bufs = {'a': [ra1, ra2, ra3], 'b': [rb1, rb2, rb3], 'c': [rc1, rc2, rc3]}
    order = ['a', 'b', 'c']

    def launch(name, stage):
        ax, at = plans[name][stage]
        n = order.index(name)
        return [copy(pick(accs[name][stage], at, turn(pos[ax], d)), bufs[name][stage].at[d - 1],
                     sends.at[n, stage, d - 1], recvs.at[n, stage, d - 1], peers[ax][d - 1]) for d in (2, 1, 3)]

    flying = {}
    for n, name in enumerate(order):
        first[n].wait_recv()
        if name == 'a':
            a0[...] = w1_ref[:, :, :, :, pl.ds(mine, q)] + r0a[...]
        elif name == 'b':
            b0[...] = w1_ref[:, :, :, :, pl.ds(pl.multiple_of(mine + q, q), q)] + r0b[...]
        else:
            c0[...] = w2_ref[:, :, :, :, pl.ds(mine, half)] + r0c[...]
        flying[name] = launch(name, 0)
    started = list(first)
    for stage in range(3):
        for name in order:
            for c in flying[name]:
                c.wait_recv()
            started += flying[name]
            ax, at = plans[name][stage]
            rb = bufs[name][stage]
            accs[name][stage + 1][...] = (pick(accs[name][stage], at, pos[ax])[...] + rb[0]) + (rb[1] + rb[2])
            if stage < 2:
                flying[name] = launch(name, stage + 1)

    rows1, rows2 = o1_ref.shape[0], o2_ref.shape[0]
    win = rows1 + rows2
    last = [copy(f1.at[pl.ds(pl.multiple_of((1 - core) * 8, 8), win)], rf1, send4.at[0], recv4.at[0], partner),
            copy(f2, rf2, send4.at[1], recv4.at[1], partner)]
    own1 = f1[pl.ds(pl.multiple_of(core * 8, 8), win), :]
    own2 = f2[...]
    for c in last:
        c.wait_recv()
    low = core == 0
    o1_ref[:, pl.ds(mine, half)] = jnp.where(low, own1[0:rows1], own1[rows2:win])
    o1_ref[:, pl.ds(his, half)] = jnp.where(low, rf1[0:rows1, :], rf1[rows2:win, :])
    o2_ref[:, pl.ds(mine, half)] = jnp.where(low, own2[0:rows2], own2[rows2:2 * rows2])
    o2_ref[:, pl.ds(his, half)] = jnp.where(low, rf2[0:rows2, :], rf2[rows2:2 * rows2, :])
    for c in started + last:
        c.wait_send()


def scatter_call(w1g, w2g):
    r1, r2, cols = w1g.shape[0] // 64, w2g.shape[0] // 64, w1g.shape[1]
    half, q = cols // 2, cols // 4
    dma = pltpu.SemaphoreType.DMA

    def f(*shape):
        return VMEM(shape, F32)

    scratch = [f(4, 4, 4, r1, q), f(4, 4, 4, r1, q), f(4, 4, 4, r2, half),
               f(4, 4, 4, r1, q), f(4, 4, 4, r1, q), f(4, 4, 4, r2, half),
               f(3, 4, 4, r1, q), f(3, 4, 4, r1, q), f(3, 4, 4, r2, half),
               f(4, 4, r1, q), f(4, 4, r1, q), f(4, 4, r2, half),
               f(3, 4, r1, q), f(3, 4, r1, q), f(3, 4, r2, half),
               f(4, r1, q), f(4, r1, q), f(4, r2, half),
               f(3, r1, q), f(3, r1, q), f(3, r2, half),
               f(r1, half), f(r2, half), f(16, half), f(r2, half),
               dma((3,)), dma((3,)), dma((3, 3, 3)), dma((3, 3, 3)), dma((2,)), dma((2,))]
    return pl.pallas_call(
        scatter_kernel,
        out_shape=(jax.ShapeDtypeStruct((r1 // 2, cols), F32), jax.ShapeDtypeStruct((r2 // 2, cols), F32)),
        in_specs=[pl.BlockSpec(memory_space=VMEM)] * 2,
        out_specs=(pl.BlockSpec(memory_space=VMEM),) * 2,
        scratch_shapes=scratch,
        compiler_params=pltpu.CompilerParams(collective_id=0, has_side_effects=True, vmem_limit_bytes=32 << 20),
        name='grad_scatter',
    )(w1g.reshape(4, 4, 4, r1, cols), w2g.reshape(4, 4, 4, r2, cols))


def bias_terms(row):
    hi = lax.reduce_precision(row, 8, 7)
    mid = lax.reduce_precision(row - hi, 8, 7)
    return [hi.astype(BF), mid.astype(BF), (row - hi - mid).astype(BF)]


def solution(mesh):
    groups = mesh.shape['graph']
    row_spec = P(('batch', 'graph'), None)
    flat_spec = P(('batch', 'graph'))
    rep_spec = P(None, None)
    down_perm = [(src_dev, src_dev - 1) for src_dev in range(1, groups)]
    up_perm = [(src_dev, src_dev + 1) for src_dev in range(groups - 1)]

    def device_step(grid_in, mesh_in, edge_in, edge_src, edge_dst, edge_mask, grid_w1, grid_w2, grid_vec,
                    mesh_w1, mesh_w2, mesh_vec, embed_w1, embed_w2, embed_vec, edge_w1, edge_w2, edge_vec,
                    node_w1, node_w2, node_vec, post_w1, post_w2, post_vec, cot_mesh, cot_grid):
        band_rows = grid_in.shape[0]
        halo_rows = band_rows // 4
        latent = grid_w2.shape[1]
        edges = edge_in.shape[0]
        band_index = lax.axis_index('graph')
        grid_y, grid_saved = mlp_forward(grid_in.astype(BF), grid_w1, grid_w2, grid_vec)
        grid_h = grid_y.astype(BF)
        from_above = lax.ppermute(grid_h[:halo_rows], 'graph', down_perm)
        from_below = lax.ppermute(grid_h[band_rows - halo_rows:], 'graph', up_perm)
        row_table = jnp.concatenate([from_below, grid_h, from_above], axis=0)
        local_src = edge_src - (band_index * band_rows - halo_rows)
        mesh_h = mlp_forward(mesh_in.astype(BF), mesh_w1, mesh_w2, mesh_vec)[0].astype(BF)
        x_aug = jnp.concatenate([edge_in.T.astype(BF), jnp.ones((3, edges), BF),
                                 jnp.zeros((9, edges), BF)], axis=0)
        wa = jnp.concatenate([embed_w1.T] + [t[:, None] for t in bias_terms(embed_vec[0])]
                             + [jnp.zeros((latent, 9), BF)], axis=1)
        dstm = jnp.where(edge_mask > 0, edge_dst, -1)
        mesh_out_t, w1_part, w2_part, tgrad_t = edge_call(
            x_aug, local_src[None], edge_dst[None], dstm[None], row_table.T, mesh_h.T, cot_mesh.T, wa,
            embed_w2.T, embed_vec.T, edge_w1.T, edge_w2.T, edge_w2, edge_vec.T,
            node_w1.T, node_w2.T, node_vec.T)
        mesh_out = mesh_out_t.T
        table_grad = tgrad_t.T
        post_y, post_saved = mlp_forward(grid_h, post_w1, post_w2, post_vec)
        grid_out = (grid_h.astype(F32) + post_y).astype(BF)
        tail_grad = lax.ppermute(table_grad[:halo_rows], 'graph', down_perm)
        head_grad = lax.ppermute(table_grad[band_rows + halo_rows:], 'graph', up_perm)
        edge_part = table_grad[halo_rows:band_rows + halo_rows] + jnp.concatenate(
            [head_grad, jnp.zeros((band_rows - 2 * halo_rows, latent), F32), tail_grad], axis=0)
        post_g1 = mlp_backward(cot_grid.astype(F32), post_w2, post_vec, post_saved)[0]
        grid_cot = cot_grid.astype(F32) + jnp.einsum('nj,kj->nk', post_g1, post_w1,
                                                     preferred_element_type=F32) + edge_part
        grid_g1 = mlp_backward(grid_cot, grid_w2, grid_vec, grid_saved)[0]
        grid_grad = jnp.einsum('nj,kj->nk', grid_g1, grid_w1, preferred_element_type=F32)
        w1_grad, w2_grad = scatter_call(w1_part, w2_part)
        return mesh_out, grid_out, grid_grad, w1_grad, w2_grad

    in_specs = (row_spec, row_spec, row_spec, flat_spec, flat_spec, flat_spec) + (rep_spec,) * 18 + (row_spec, row_spec)
    return jax.shard_map(device_step, mesh=mesh, in_specs=in_specs, out_specs=(row_spec,) * 5, check_vma=False)
```

time: 1010 us -> 212 us (0.21)
  blocking collectives: 336 us -> 0 us
  other arithmetic: 165 us -> 8.23 us
  Pallas kernels: 0 us -> 153 us
  local copies, waits for them, and re-layouts: 165 us -> 22.7 us
  matrix products: 121 us -> 14.4 us
  starting transfers between devices: 105 us -> 12 us
  waiting for transfers between devices: 90.8 us -> 0.01 us
  between operations: 16 us -> 1.19 us
    unnamed x1 -> x0, blocking collectives: 336 us -> none
    pallas_call x0 -> x2, Pallas kernels: none -> 153 us  [the longest x1 118 us: edge_call(): pl.pallas_call(edge_kernel, out_shape=out_shape, in_specs=[pl.BlockSpec(m...]
    scatter-add x2 -> x0, other arithmetic: 111 us -> none  [the longest x1 61 us: device_step(): jax.ops.segment_sum(message, edge_dst, num_segments=mesh_rows)]
    dot_general x17 -> x7, matrix products: 121 us -> 14.4 us  [the longest x1 5.28 us: device_step(): jnp.einsum('nj,kj->nk', post_g1, post_w1, preferred_element_type=F32)]
    gather x3 -> x0, local copies, waits for them, and re-layouts: 99.9 us -> none  [the longest x1 33.6 us: device_step(): row_table[local_src]]
    unnamed x33 -> x0, starting transfers between devices: 93.7 us -> none
    unnamed x34 -> x0, waiting for transfers between devices: 90.8 us -> none
    unnamed x124 -> x100, local copies, waits for them, and re-layouts: 61 us -> 17.4 us
  transfers between devices with their start and end apart: 37 -> 4, of which waited for: 1 -> 0; matrix products, arithmetic and copies ran while one was open for 21% -> 13% of each run, Pallas kernels for 0% -> 16%
where the time goes in v1:
time: 212 us; the launch traced here: 211 us
  Pallas kernels  153 us (72%)
  local copies, waits for them, and re-layouts  22.7 us (11%)
  matrix products  14.4 us (7%)
  starting transfers between devices  12 us (6%)
  other arithmetic  8.23 us (4%)
    pallas_call x1, Pallas kernels, edge_call(): pl.pallas_call(edge_kernel, out_shape=out_shape, in_specs=[pl.BlockSpec(m...  118 us
    pallas_call x1, Pallas kernels, scatter_call(): pl.pallas_call(scatter_kernel, out_shape=(jax.ShapeDtypeStruct((r1 // 2,...  34.2 us
    unnamed x100, local copies, waits for them, and re-layouts  17.4 us
    dot_general x1, matrix products, device_step(): jnp.einsum('nj,kj->nk', post_g1, post_w1, preferred_element_type=F32)  5.28 us
    ppermute x1, starting transfers between devices, device_step(): from_below = lax.ppermute(grid_h[band_rows - halo_rows:], 'graph', up_perm)  4.49 us
    dot_general x3, matrix products, mlp_forward(): pre_two = jnp.dot(act_bf, w_two, preferred_element_type=F32) + vec_rows[1]  4.43 us
  transfers between devices with their start and end apart: 4, of which 0 were waited for; matrix products, arithmetic and copies ran while one was open for 13% of the time, Pallas kernels for 16%

profile of v1, /device:TPU:1, one launch (start us, length us, event | category | flops | bytes accessed | tf_op | source)
XLA Modules:
  0.0 211.1 jit_solution(1361493545463991974)
XLA Ops:
  1.5 1.4 convolution_add_fusion.4
  5.0 4.5 %collective-permute-start = (bf16[128,512]{0,1:T(8,128)(2,1)}, bf16[128,512]{0,1:T(8,128)(2,1)S(1)}, u32[]{:S(2)}, u32[]{:S(2)}) collective-permute-start(bf16[128,512]{0,1:T(8,128)(2,1)} %get-tuple-element.39), channel_id=1, source_target_pairs={{0,1},{1,2},{2,3},{3,4},{4,5},{5,6},{6,7},{7,8},{8,9},{9,10},{10,1... | collective-permute-start | bytes 393224 | tf_op jit(solution)/shard_map/ppermute | solution.py:329
  9.5 1.9 collective-permute-start.1
  12.4 1.8 fusion.63
  15.5 1.6 copy.65
  17.1 2.4 %copy.68 = bf16[1024,512]{0,1:T(8,128)(2,1)} copy(bf16[1024,512]{1,0:T(8,128)(2,1)} %param.44) | data formatting | bytes 2097152 | tf_op args[18]
  19.4 1.0 copy.63
  20.5 1.0 copy.66
  21.5 1.0 copy.69
  23.5 0.9 copy.67
  26.4 2.0 fusion.66
  28.5 1.2 copy.72
  31.0 0.9 fusion.44.hm_ref
  33.3 1.0 maximum_bitcast_fusion.table_ref
  34.3 118.3 %edge_pass.1 = (bf16[512,256]{1,0:T(8,128)(2,1)}, f32[1536,512]{1,0:T(8,128)}, f32[512,512]{1,0:T(8,128)}, f32[512,768]{1,0:T(8,128)}) custom-call(bf16[16,8192]{1,0:T(8,128)(2,1)} %maximum_maximum_fusion.x_ref, s32[1,8192]{1,0:T(1,128)} %bitcast.69, s32[1,8192]{1,0:T(1,128)} %bitcast.67, s32[1,8192]{1,0:T(1,128)} %bitcast.68, ...), custom_call_target="tpu_custom_call" | custom-call | tf_op jit(solution)/shard_map/edge_pass/pallas_call | solution.py:165
  152.7 1.9 fusion.57
  154.6 3.6 %collective-permute-start.2 = (f32[128,512]{0,1:T(8,128)}, f32[128,512]{0,1:T(8,128)}, u32[]{:S(2)}, u32[]{:S(2)}) collective-permute-start(f32[128,512]{0,1:T(8,128)} %get-tuple-element.36), channel_id=1, source_target_pairs={{0,1},{1,2},{2,3},{3,4},{4,5},{5,6},{6,7},{7,8},{8,9},{9,10},{10,1... | collective-permute-start | bytes 786440 | tf_op jit(solution)/shard_map/ppermute | solution.py:347
  158.3 1.9 collective-permute-start.3
  160.2 2.9 %fusion.4 = (f32[512]{0:T(512)S(1)}, f32[512]{0:T(512)S(1)}, bf16[512,512]{0,1:T(8,128)(2,1)}) fusion(bf16[512,512]{0,1:T(8,128)(2,1)} %copy.72, f32[512]{0:T(512)} %bitcast.75, f32[512]{0:T(512)} %add_rsqrt_fusion, f32[512,512]{0,1:T(8,128)} %copy-done.5, f32[512]{0:T(512)} %copy-done.26, f32[512]{0:T(512)} %bitcast.77, f32[512]{0:T(512)} %bitcast.74, ...), kind=kLoop, calls=%fused_computation.12 | loop fusion | flops 4455424 | bytes 3166208 | tf_op jit(solution)/shard_map/reduce_sum | solution.py:30
  163.2 2.0 copy.74
  165.2 1.2 copy-done.1
  166.5 34.2 %grad_scatter.1 = (f32[12,512]{1,0:T(8,128)S(1)}, f32[4,512]{1,0:T(4,128)S(1)}) custom-call(f32[4,4,4,24,512]{4,3,2,1,0:T(8,128)S(1)} %bitcast.53, f32[4,4,4,8,512]{4,3,2,1,0:T(8,128)S(1)} %bitcast.54), custom_call_target="tpu_custom_call" | custom-call | tf_op jit(solution)/shard_map/grad_scatter/pallas_call | solution.py:293
  201.7 5.3 %fusion.56 = (f32[512]{0:T(512)S(1)}, f32[512]{0:T(512)S(1)}, f32[512,512]{0,1:T(8,128)}) fusion(f32[512]{0:T(512)S(1)} %copy-done.25, f32[512,512]{0,1:T(8,128)} %copy-done.2, f32[512]{0:T(512)S(1)} %copy-done.21, f32[512]{0:T(512)S(1)} %bitcast.72, f32[128,512]{0,1:T(8,128)} %collective-permute-done.3, f32[512]{0:T(512)S(1)} %pad.1.clone, ...), kind=kOutput, calls=%fused_computation.89 | convolution fusion | flops 544734208 | bytes 7886848 | tf_op jit(solution)/shard_map/nj,kj->nk/dot_general | solution.py:351
  207.0 2.9 %fusion.7 = f32[512,186]{0,1:T(8,128)} fusion(bf16[186,512]{1,0:T(8,128)(2,1)S(1)} %copy-done.17, bf16[512,512]{1,0:T(8,128)(2,1)S(1)} %copy-done.40, f32[512,512]{1,0:T(8,128)S(1)} %copy-done.9, f32[512,512]{0,1:T(8,128)} %get-tuple-element.62, f32[512,512]{0,1:T(8,128)S(1)} %copy-done.4, f32[512]{0:T(512)S(1)} %broadcast_multiply_fusion, ...), kind=kOutput, calls=%fused_computation.15 | convolution fusion | flops 370147328 | bytes 4249600 | tf_op jit(solution)/shard_map/nj,kj->nk/dot_general | solution.py:354
  (128 shorter events, 13.0 us)
Async XLA Ops:
  3.9 7.6 %copy-start.31 = (f32[4,512]{1,0:T(4,128)S(1)}, f32[4,512]{1,0:T(4,128)}, u32[]{:S(2)}) copy-start(f32[4,512]{1,0:T(4,128)} %param.40) | copy-start | bytes 24580
  3.9 8.5 %copy-start.36 = (f32[4,512]{1,0:T(4,128)S(1)}, f32[4,512]{1,0:T(4,128)}, u32[]{:S(2)}) copy-start(f32[4,512]{1,0:T(4,128)} %param.37) | copy-start | bytes 24580
  3.9 8.5 %copy-start.41 = (bf16[3,512]{1,0:T(4,128)(2,1)S(1)}, bf16[3,512]{1,0:T(4,128)(2,1)}, u32[]{:S(2)}) copy-start(bf16[3,512]{1,0:T(4,128)(2,1)} %param.35) | copy-start | bytes 9220
  3.9 8.5 %copy-start.42 = (f32[256,3]{0,1:T(4,128)S(1)}, f32[256,3]{0,1:T(4,128)}, u32[]{:S(2)}) copy-start(f32[256,3]{0,1:T(4,128)} %param.27) | copy-start | bytes 9220
  4.1 7.3 %copy-start.24 = (f32[512]{0:T(512)}, f32[512]{0:T(512)S(1)}, u32[]{:S(2)}) copy-start(f32[512]{0:T(512)S(1)} %add_rsqrt_fusion.1) | copy-start | bytes 6148
  5.0 28.3 %collective-permute-start = (bf16[128,512]{0,1:T(8,128)(2,1)}, bf16[128,512]{0,1:T(8,128)(2,1)S(1)}, u32[]{:S(2)}, u32[]{:S(2)}) collective-permute-start(bf16[128,512]{0,1:T(8,128)(2,1)} %get-tuple-element.39), channel_id=1, source_target_pairs={{0,1},{1,2},{2,3},{3,4},{4,5},{5,6},{6,7},{7,8},{8,9},{9,10},{10,1... | collective-permute-start | bytes 393224 | tf_op jit(solution)/shard_map/ppermute | solution.py:329
  9.5 23.8 %collective-permute-start.1 = (bf16[128,512]{0,1:T(8,128)(2,1)S(1)}, bf16[128,512]{0,1:T(8,128)(2,1)S(1)}, u32[]{:S(2)}, u32[]{:S(2)}) collective-permute-start(bf16[128,512]{0,1:T(8,128)(2,1)S(1)} %get-tuple-element.40), channel_id=1, source_target_pairs={{1,0},{2,1},{3,2},{4,3},{5,4},{6,5},{7,6},{8,7},{9,8},{10,9},{11,1... | collective-permute-start | bytes 393224 | tf_op jit(solution)/shard_map/ppermute | solution.py:328
  20.5 4.8 %copy-start.37 = (f32[4,512]{1,0:T(4,128)S(1)}, f32[4,512]{1,0:T(4,128)}, u32[]{:S(2)}) copy-start(f32[4,512]{1,0:T(4,128)} %param.49) | copy-start | bytes 24580
  20.5 5.4 %copy-start.11 = (bf16[512,512]{1,0:T(8,128)(2,1)S(1)}, bf16[512,512]{1,0:T(8,128)(2,1)}, u32[]{:S(2)}) copy-start(bf16[512,512]{1,0:T(8,128)(2,1)} %param.47) | copy-start | bytes 1572868
  152.7 7.5 %copy-start.3 = (f32[512,512]{0,1:T(8,128)S(1)}, f32[512,512]{0,1:T(8,128)}, u32[]{:S(2)}) copy-start(f32[512,512]{0,1:T(8,128)} %copy-done.2) | copy-start | bytes 3145732
  154.6 47.0 %collective-permute-start.2 = (f32[128,512]{0,1:T(8,128)}, f32[128,512]{0,1:T(8,128)}, u32[]{:S(2)}, u32[]{:S(2)}) collective-permute-start(f32[128,512]{0,1:T(8,128)} %get-tuple-element.36), channel_id=1, source_target_pairs={{0,1},{1,2},{2,3},{3,4},{4,5},{5,6},{6,7},{7,8},{8,9},{9,10},{10,1... | collective-permute-start | bytes 786440 | tf_op jit(solution)/shard_map/ppermute | solution.py:347
  158.3 43.3 %collective-permute-start.3 = (f32[128,512]{0,1:T(8,128)}, f32[128,512]{0,1:T(8,128)}, u32[]{:S(2)}, u32[]{:S(2)}) collective-permute-start(f32[128,512]{0,1:T(8,128)} %get-tuple-element.37), channel_id=1, source_target_pairs={{1,0},{2,1},{3,2},{4,3},{5,4},{6,5},{7,6},{8,7},{9,8},{10,9},{11,1... | collective-permute-start | bytes 786440 | tf_op jit(solution)/shard_map/ppermute | solution.py:346
  160.2 5.0 %copy-start = (f32[1536,512]{1,0:T(8,128)S(1)}, f32[1536,512]{1,0:T(8,128)}, u32[]{:S(2)}) copy-start(f32[1536,512]{1,0:T(8,128)} %get-tuple-element.13) | copy-start | bytes 9437188
  166.5 34.3 %copy-start.16 = (bf16[512,256]{1,0:T(8,128)(2,1)S(1)}, bf16[512,256]{1,0:T(8,128)(2,1)}, u32[]{:S(2)}) copy-start(bf16[512,256]{1,0:T(8,128)(2,1)} %get-tuple-element.11) | copy-start | bytes 786436
  166.5 35.1 %copy-start.21 = (f32[512]{0:T(512)S(1)}, f32[512]{0:T(512)}, u32[]{:S(2)}) copy-start(f32[512]{0:T(512)} %copy-done.20) | copy-start | bytes 6148
  166.5 35.1 %copy-start.25 = (f32[512]{0:T(512)S(1)}, f32[512]{0:T(512)}, u32[]{:S(2)}) copy-start(f32[512]{0:T(512)} %copy-done.24) | copy-start | bytes 6148
  166.5 35.1 %copy-start.27 = (f32[512]{0:T(512)S(1)}, f32[512]{0:T(512)}, u32[]{:S(2)}) copy-start(f32[512]{0:T(512)} %copy-done.26) | copy-start | bytes 6148
  166.5 35.1 %copy-start.29 = (f32[1,512]{1,0:T(1,128)S(1)}, f32[1,512]{1,0:T(1,128)}, u32[]{:S(2)}) copy-start(f32[1,512]{1,0:T(1,128)} %copy-done.28) | copy-start | bytes 6148
  166.5 35.1 %copy-start.32 = (f32[512]{0:T(512)S(1)}, f32[512]{0:T(512)}, u32[]{:S(2)}) copy-start(f32[512]{0:T(512)} %add_rsqrt_fusion) | copy-start | bytes 6148
  166.5 35.1 %copy-start.33 = (f32[1,512]{1,0:T(1,128)S(1)}, f32[1,512]{1,0:T(1,128)}, u32[]{:S(2)}) copy-start(f32[1,512]{1,0:T(1,128)} %get-tuple-element.41) | copy-start | bytes 6148
  201.7 5.3 %copy-start.4 = (f32[512,512]{0,1:T(8,128)S(1)}, f32[512,512]{0,1:T(8,128)}, u32[]{:S(2)}) copy-start(f32[512,512]{0,1:T(8,128)} %copy-done.2) | copy-start | bytes 3145732
  201.7 5.3 %copy-start.9 = (f32[512,512]{1,0:T(8,128)S(1)}, f32[512,512]{1,0:T(8,128)}, u32[]{:S(2)}) copy-start(f32[512,512]{1,0:T(8,128)} %copy-done.8) | copy-start | bytes 3145732
  201.7 5.3 %copy-start.17 = (bf16[186,512]{1,0:T(8,128)(2,1)S(1)}, bf16[186,512]{1,0:T(8,128)(2,1)}, u32[]{:S(2)}) copy-start(bf16[186,512]{1,0:T(8,128)(2,1)} %param.32) | copy-start | bytes 571396
  201.7 5.3 %copy-start.40 = (bf16[512,512]{1,0:T(8,128)(2,1)S(1)}, bf16[512,512]{1,0:T(8,128)(2,1)}, u32[]{:S(2)}) copy-start(bf16[512,512]{1,0:T(8,128)(2,1)} %param.33) | copy-start | bytes 1572868
  (23 other events, 62.0 us)

commit v2 on v0

v2 whole, which is shorter than its diff:
```python
import jax
import jax.numpy as jnp
from jax import lax
from jax.experimental import pallas as pl
from jax.experimental.pallas import tpu as pltpu
from jax.sharding import PartitionSpec as P

NORM_EPS = 1e-5
BF = jnp.bfloat16
F32 = jnp.float32
VMEM = pltpu.VMEM
CHUNK = 512
FETCHED = (10, 13, 15, 21, 22, 25)
DEV = pl.DeviceIdType.MESH
GRID, MESH, EMBED, EDGE, NODE, POST = range(6)


def dot_nn(a, b):
    return jnp.dot(a, b, preferred_element_type=F32)


def dot_nt(a, b):
    return lax.dot_general(a, b, (((1,), (1,)), ((), ())), preferred_element_type=F32)


def dot_tn(a, b):
    return lax.dot_general(a, b, (((0,), (0,)), ((), ())), preferred_element_type=F32)


def split3(x):
    hi = x.astype(BF)
    rest = x - hi.astype(F32)
    mid = rest.astype(BF)
    low = (rest - mid.astype(F32)).astype(BF)
    return [hi, mid, low]


def silu_bf(p):
    h = 0.5 * p
    return (h + h * jnp.tanh(h)).astype(BF)


def norm_cols(q):
    centred = q - jnp.mean(q, axis=0, keepdims=True)
    inv = lax.rsqrt(jnp.mean(centred * centred, axis=0, keepdims=True) + NORM_EPS)
    return centred * inv, inv


def norm_back(d, n, inv):
    return inv * (d - jnp.mean(d, axis=0, keepdims=True) - n * jnp.mean(d * n, axis=0, keepdims=True))


def grad_first(d_act, p):
    t = jnp.tanh(0.5 * p)
    s = 0.5 + 0.5 * t
    return (d_act * (s * (1.0 + p * (1.0 - s)))).astype(BF)


def one_hot(rows, idx):
    return (lax.broadcasted_iota(jnp.int32, (rows, idx.shape[1]), 0) == idx).astype(F32).astype(BF)


def lanes(*parts):
    return jnp.concatenate(parts, axis=1)


def rows(*parts):
    return jnp.concatenate(parts, axis=0)


def step_kernel(gx_ref, mx_ref, ex_ref, src_ref, dst_ref, mask_ref,
                gw1_ref, gw2_ref, gvec_ref, mw1_ref, mw2_ref, mvec_ref, ew1_ref, ew2_ref, evec_ref,
                dw1_ref, dw2_ref, dvec_ref, nw1_ref, nw2_ref, nvec_ref, pw1_ref, pw2_ref, pvec_ref,
                cotm_ref, cotg_ref,
                mesh_out_ref, grid_out_ref, ggrad_ref, o1_ref, o2_ref,
                pre_s, norm_s, he_s, inv_s, wl_s, bt_s, agg_s, w1g_s, w2g_s, table_s, hm_s, ew2t_s, dw2t_s, v_s, vt_s,
                stage_sem, done_sem, hs_sem, hr_sem, ts_sem, tr_sem, send0, recv0, sends, recvs, send4, recv4):
    lat = dw2_ref.shape[0]
    band = gx_ref.shape[1]
    nm = mx_ref.shape[1]
    halo = band // 4
    nt = band + 2 * halo
    ch = he_s.shape[1]
    steps = he_s.shape[0] // lat

    me = lax.axis_index('graph')
    total = 128
    core = lax.rem(me, 2)
    chip = me // 2
    px, py, pz = lax.rem(chip, 4), lax.rem(chip // 4, 4), chip // 16

    def dev(z, y, x, k):
        return {'graph': ((z * 4 + y) * 4 + x) * 2 + k}

    def turn(v, d):
        return lax.rem(v + d, 4)

    below = {'graph': lax.rem(me + total - 1, total)}
    above = {'graph': lax.rem(me + 1, total)}
    partner = dev(pz, py, px, 1 - core)
    peers = {'x': [dev(pz, py, turn(px, d), core) for d in (1, 2, 3)],
             'y': [dev(pz, turn(py, d), px, core) for d in (1, 2, 3)],
             'z': [dev(turn(pz, d), py, px, core) for d in (1, 2, 3)]}
    pos = {'x': px, 'y': py, 'z': pz}
    everyone = [below, above, partner] + peers['x'] + peers['y'] + peers['z']

    def fetch(k, src, slot):
        n = src.shape[0]
        c = pltpu.make_async_copy(src, he_s.at[slot * lat:slot * lat + n, :], stage_sem.at[k])
        c.start()
        return c

    def held(slot, n=1):
        return he_s[slot * lat:(slot + n) * lat, :]

    early = [fetch(0, mw2_ref, 15), fetch(1, dw1_ref, 10), fetch(2, ew2_ref, 14)]

    barrier = pltpu.get_barrier_semaphore()
    for peer in everyone:
        pl.semaphore_signal(barrier, inc=1, device_id=peer, device_id_type=DEV)

    def copy(src, dst, ssem, rsem, peer):
        c = pltpu.make_async_remote_copy(src_ref=src, dst_ref=dst, send_sem=ssem, recv_sem=rsem, device_id=peer,
                                         device_id_type=DEV)
        c.start()
        return c

    v_s[...] = jnp.zeros_like(v_s)
    for k, ref in enumerate((gvec_ref, mvec_ref, evec_ref, dvec_ref, nvec_ref, pvec_ref)):
        v_s[4 * k:4 * k + 4, :] = ref[...]
    vt_s[...] = v_s[...].T

    def col(mlp, k):
        return vt_s[:, 4 * mlp + k:4 * mlp + k + 1]

    def scaled(n, mlp):
        return n * col(mlp, 2) + col(mlp, 3)

    def grid_forward():
        p = dot_tn(gw1_ref[...], gx_ref[...].astype(BF)) + col(GRID, 0)
        n, inv = norm_cols(dot_tn(gw2_ref[...], silu_bf(p)) + col(GRID, 1))
        return p, n, inv

    table_s[:, halo:halo + band] = scaled(grid_forward()[1], GRID).astype(BF)
    pl.semaphore_wait(barrier, len(everyone))
    halos = [copy(table_s.at[:, halo:2 * halo], table_s.at[:, halo + band:nt], hs_sem.at[0], hr_sem.at[0], below),
             copy(table_s.at[:, band:band + halo], table_s.at[:, 0:halo], hs_sem.at[1], hr_sem.at[1], above)]

    for c in early:
        c.wait()
    mp = dot_tn(mw1_ref[...], mx_ref[...].astype(BF)) + col(MESH, 0)
    mn, _ = norm_cols(dot_tn(held(15), silu_bf(mp)) + col(MESH, 1))
    hm_s[...] = scaled(mn, MESH).astype(BF)

    wl_s[:, 0:lat] = held(10).T
    wl_s[:, lat:2 * lat] = held(11).T
    ew2t_s[...] = held(14).T
    dw2t_s[...] = dw2_ref[...].T
    pm = dot_tn(held(12), hm_s[...]) + col(EDGE, 0)
    for k, part in enumerate(split3(pm)):
        wl_s[:, 2 * lat + k * nm:2 * lat + (k + 1) * nm] = part
    agg_s[...] = jnp.zeros_like(agg_s)
    base = me * band - halo

    def slab(i):
        return pl.ds(pl.multiple_of(i * ch, ch), ch)

    def masked_dst(sl):
        return jnp.where(mask_ref[:, sl] > 0, dst_ref[:, sl], -1)

    def embed(i):
        pe = dot_tn(ew1_ref[...], ex_ref[:, slab(i)].astype(BF)) + col(EMBED, 0)
        ne, _ = norm_cols(dot_nn(ew2t_s[...], silu_bf(pe)) + col(EMBED, 1))
        he_s[slab(i), :] = scaled(ne, EMBED).astype(BF)

    def first_half(i):
        sl = slab(i)
        gath = dot_nn(table_s[...], one_hot(nt, src_ref[:, sl] - base)).astype(BF)
        ohd = one_hot(nm, dst_ref[:, sl])
        pre_s[sl, :] = dot_nn(wl_s[...], rows(he_s[sl, :], gath, ohd, ohd, ohd))

    def second_half(i):
        sl = slab(i)
        n, inv = norm_cols(dot_nn(dw2t_s[...], silu_bf(pre_s[sl, :])) + col(EDGE, 1))
        norm_s[sl, :] = n
        inv_s[i] = inv
        msg = he_s[sl, :].astype(F32) + scaled(n, EDGE)
        ohm = one_hot(nm, masked_dst(sl))
        agg_s[...] += dot_nt(lanes(*split3(msg)), lanes(ohm, ohm, ohm))

    def fwd(i, carry):
        second_half(i - 1)
        first_half(i)
        embed(jnp.minimum(i + 1, steps - 1))
        return carry

    embed(0)
    embed(1)
    for c in halos:
        c.wait_recv()
    first_half(0)
    lax.fori_loop(1, steps, fwd, 0)
    second_half(steps - 1)

    hm = hm_s[...]
    np_ = dot_tn(nw1_ref[...], rows(hm, agg_s[...].astype(BF))) + col(NODE, 0)
    nn_, ninv = norm_cols(dot_tn(nw2_ref[...], silu_bf(np_)) + col(NODE, 1))
    mesh_out_ref[...] = (hm.astype(F32) + scaled(nn_, NODE)).T.astype(BF)
    d2 = norm_back(cotm_ref[...].astype(F32).T * col(NODE, 2), nn_, ninv)
    ng1 = grad_first(dot_nn(nw2_ref[...], d2.astype(BF)), np_)
    ag = dot_nn(nw1_ref[lat:2 * lat, :], ng1) * col(EDGE, 2)
    ag = ag - jnp.mean(ag, axis=0, keepdims=True)
    for k, part in enumerate(split3(ag)):
        bt_s[:, k * nm:(k + 1) * nm] = part

    w1g_s[...] = jnp.zeros_like(w1g_s)
    w2g_s[...] = jnp.zeros_like(w2g_s)

    def bwd(i, carry):
        sl = slab(i)
        ohm = one_hot(nm, masked_dst(sl))
        bg = dot_nn(bt_s[...], rows(ohm, ohm, ohm))
        n = norm_s[sl, :]
        g2 = (inv_s[i] * (bg - n * jnp.mean(bg * n, axis=0, keepdims=True))).astype(BF)
        p = pre_s[sl, :]
        w2g_s[...] += dot_nt(silu_bf(p), g2)
        g1 = grad_first(dot_nn(dw2_ref[...], g2), p)
        w1g_s[...] += dot_nt(rows(he_s[sl, :], one_hot(nt, src_ref[:, sl] - base), ohm), g1)
        return carry

    lax.fori_loop(0, steps, bwd, 0)

    for peer in everyone:
        pl.semaphore_signal(done_sem, inc=1, device_id=peer, device_id_type=DEV)
    late = [fetch(3, dw1_ref.at[lat:2 * lat, :], 8), fetch(4, pw1_ref, 5), fetch(5, pw2_ref, 6), fetch(6, cotg_ref, 7)]
    for k, part in enumerate(split3(w1g_s[lat:lat + nt, :])):
        he_s[k * nt:(k + 1) * nt, :] = part
    t0 = 9 * lat
    for k, part in enumerate(split3(w1g_s[lat + nt:lat + nt + nm, :])):
        he_s[t0 + k * nm:t0 + (k + 1) * nm, :] = part
    for c in late:
        c.wait()
    wb = held(8)
    tg = dot_nt(lanes(wb, wb, wb), lanes(he_s[0:nt, :], he_s[nt:2 * nt, :], he_s[2 * nt:3 * nt, :]))
    norm_s[0:lat, 0:halo] = tg[:, 0:halo]
    norm_s[0:lat, halo:2 * halo] = tg[:, halo + band:nt]
    norm_s[lat:2 * lat, :] = tg[:, halo:halo + band]
    pl.semaphore_wait(done_sem, len(everyone))
    tails = [copy(norm_s.at[0:lat, 0:halo], pre_s.at[0:lat, 2 * halo:3 * halo], ts_sem.at[0], tr_sem.at[0], below),
             copy(norm_s.at[0:lat, halo:2 * halo], pre_s.at[0:lat, 3 * halo:4 * halo], ts_sem.at[1], tr_sem.at[1],
                  above)]
    half = lat // 2
    q = half // 2
    mine = pl.multiple_of(core * half, half)
    his = pl.multiple_of((1 - core) * half, half)
    n1, n2 = 3 * lat, lat
    first = {'c': copy(w2g_s.at[:, pl.ds(his, half)], pre_s.at[n1:n1 + n2, 0:half], send0.at[2], recv0.at[2], partner)}
    tb = table_s[...]
    w1g_s[lat:2 * lat, :] = dot_nn(lanes(tb, tb, tb), he_s[0:3 * nt, :])
    w1g_s[2 * lat:3 * lat, :] = dot_nn(lanes(hm, hm, hm), he_s[t0:t0 + 3 * nm, :])
    first['a'] = copy(w1g_s.at[:, pl.ds(his, q)], pre_s.at[0:n1, 0:q], send0.at[0], recv0.at[0], partner)
    first['b'] = copy(w1g_s.at[:, pl.ds(pl.multiple_of(his + q, q), q)], pre_s.at[0:n1, q:half], send0.at[1],
                      recv0.at[1], partner)

    gp, gn, ginv = grid_forward()
    keep_p, keep_n = slice(10 * lat, 11 * lat), slice(11 * lat, 12 * lat)
    norm_s[keep_p, :] = gp
    norm_s[keep_n, :] = gn
    inv_s[0] = ginv
    hg = table_s[:, halo:halo + band]
    pp = dot_tn(held(5), hg) + col(POST, 0)
    pn, pinv = norm_cols(dot_tn(held(6), silu_bf(pp)) + col(POST, 1))
    grid_out_ref[...] = (hg.astype(F32) + scaled(pn, POST)).T.astype(BF)
    cg = held(7).astype(F32).T
    pd = norm_back(cg * col(POST, 2), pn, pinv)
    pg1 = grad_first(dot_nn(held(6), pd.astype(BF)), pp)
    norm_s[2 * lat:3 * lat, :] = cg + dot_nn(held(5), pg1)

    b1, b2 = n1 // 64, n2 // 64
    shape = {'a': (b1, 0, q), 'b': (b1, q, q), 'c': (b2, 0, half)}
    axes = {'a': 'xyz', 'b': 'yzx', 'c': 'zxy'}
    order = 'cab'
    at = {'a': 0, 'b': 0, 'c': 64 * b1}
    acc_rows = {k: [] for k in order}
    buf_rows = {k: [] for k in order}
    top_a, top_b = 4 * lat, n1 + n2
    for stage in range(4):
        for k in 'ac':
            acc_rows[k].append(top_a)
            top_a += shape[k][0] * 4 ** (3 - stage)
            buf_rows[k].append(top_b)
            top_b += 0 if stage == 3 else 3 * shape[k][0] * 4 ** (2 - stage)
    acc_rows['b'], buf_rows['b'] = acc_rows['a'], buf_rows['a']

    def acc_at(k, stage, off, n):
        return norm_s.at[pl.ds(acc_rows[k][stage] + off, n), shape[k][1]:shape[k][1] + shape[k][2]]

    def buf_at(k, stage, slot, n):
        return pre_s.at[pl.ds(buf_rows[k][stage] + slot * n, n), shape[k][1]:shape[k][1] + shape[k][2]]

    def launch(k, stage):
        n = shape[k][0] * 4 ** (2 - stage)
        ax = axes[k][stage]
        j = order.index(k)
        return [copy(acc_at(k, stage, pl.multiple_of(turn(pos[ax], d) * n, 8), n), buf_at(k, stage, d - 1, n),
                     sends.at[j, stage, d - 1], recvs.at[j, stage, d - 1], peers[ax][d - 1]) for d in (2, 1, 3)]

    flying = {}
    for k in order:
        n, c0, w = shape[k]
        first[k].wait_recv()
        src = w2g_s if k == 'c' else w1g_s
        for i in range(64):
            v = {'z': i // 16, 'y': i // 4 % 4, 'x': i % 4}
            to = (v[axes[k][0]] * 4 + v[axes[k][1]]) * 4 + v[axes[k][2]]
            acc_at(k, 0, to * n, n)[...] = (src[i * n:(i + 1) * n, pl.ds(pl.multiple_of(mine + c0, q), w)]
                                            + pre_s[at[k] + i * n:at[k] + (i + 1) * n, c0:c0 + w])
        flying[k] = launch(k, 0)
    started = tails + halos + [first[k] for k in order]

    for c in tails:
        c.wait_recv()
    own = norm_s[2 * lat:3 * lat, :] + norm_s[lat:2 * lat, :]
    ends = lanes(own[:, 0:halo] + pre_s[0:lat, 3 * halo:4 * halo], own[:, halo:band - halo],
                 own[:, band - halo:band] + pre_s[0:lat, 2 * halo:3 * halo])
    gd = norm_back(ends * col(GRID, 2), norm_s[keep_n, :], inv_s[0])
    gg1 = grad_first(dot_nn(gw2_ref[...], gd.astype(BF)), norm_s[keep_p, :])
    ggrad_ref[...] = dot_nn(gw1_ref[...], gg1)

    for stage in range(3):
        for k in order:
            for c in flying[k]:
                c.wait_recv()
            started += flying[k]
            n = shape[k][0] * 4 ** (2 - stage)
            keep = acc_at(k, stage, pl.multiple_of(pos[axes[k][stage]] * n, 8), n)[...]
            acc_at(k, stage + 1, 0, n)[...] = (keep + buf_at(k, stage, 0, n)[...]) + (
                buf_at(k, stage, 1, n)[...] + buf_at(k, stage, 2, n)[...])
            if stage < 2:
                flying[k] = launch(k, stage + 1)

    r1, r2 = o1_ref.shape[0], o2_ref.shape[0]
    win = r1 + r2
    f1, f2 = acc_rows['a'][3], acc_rows['c'][3]
    e1, e2 = top_b, top_b + win
    last = [copy(norm_s.at[pl.ds(pl.multiple_of(f1 + (1 - core) * 8, 8), win), 0:half], pre_s.at[e1:e1 + win, 0:half],
                 send4.at[0], recv4.at[0], partner),
            copy(norm_s.at[f2:f2 + b2, 0:half], pre_s.at[e2:e2 + b2, 0:half], send4.at[1], recv4.at[1], partner)]
    own1 = norm_s[pl.ds(pl.multiple_of(f1 + core * 8, 8), win), 0:half]
    own2 = norm_s[f2:f2 + b2, 0:half]
    low = core == 0
    o1_ref[:, pl.ds(mine, half)] = jnp.where(low, own1[0:r1], own1[r2:win])
    o2_ref[:, pl.ds(mine, half)] = jnp.where(low, own2[0:r2], own2[r2:b2])
    for c in last:
        c.wait_recv()
    got1 = pre_s[e1:e1 + win, 0:half]
    got2 = pre_s[e2:e2 + b2, 0:half]
    o1_ref[:, pl.ds(his, half)] = jnp.where(low, got1[0:r1], got1[r2:win])
    o2_ref[:, pl.ds(his, half)] = jnp.where(low, got2[0:r2], got2[r2:b2])
    for c in started + last:
        c.wait_send()


def step_call(args, sizes):
    band, nm, edges, lat, feats = sizes
    steps = edges // CHUNK
    nt = band + band // 2
    dma = pltpu.SemaphoreType.DMA
    out_shape = (jax.ShapeDtypeStruct((nm, lat), BF), jax.ShapeDtypeStruct((band, lat), BF),
                 jax.ShapeDtypeStruct((feats, band), F32), jax.ShapeDtypeStruct((3 * lat // 128, lat), F32),
                 jax.ShapeDtypeStruct((lat // 128, lat), F32))
    return pl.pallas_call(
        step_kernel,
        out_shape=out_shape,
        in_specs=[pl.BlockSpec(memory_space=pl.ANY if k in FETCHED else VMEM) for k in range(len(args))],
        out_specs=(pl.BlockSpec(memory_space=VMEM),) * len(out_shape),
        scratch_shapes=[VMEM((edges, CHUNK), F32), VMEM((edges, CHUNK), F32), VMEM((steps * lat, CHUNK), BF),
                        VMEM((steps, 1, CHUNK), F32), VMEM((lat, 2 * lat + 3 * nm), BF), VMEM((lat, 3 * nm), BF),
                        VMEM((lat, nm), F32), VMEM((3 * lat, lat), F32), VMEM((lat, lat), F32), VMEM((lat, nt), BF),
                        VMEM((lat, nm), BF), VMEM((lat, lat), BF), VMEM((lat, lat), BF),
                        VMEM((128, lat), F32), VMEM((lat, 128), F32),
                        dma((7,)), pltpu.SemaphoreType.REGULAR, dma((2,)), dma((2,)), dma((2,)), dma((2,)),
                        dma((3,)), dma((3,)), dma((3, 3, 3)), dma((3, 3, 3)), dma((2,)), dma((2,))],
        compiler_params=pltpu.CompilerParams(collective_id=0, has_side_effects=True, vmem_limit_bytes=67043328),
        name='whole_step',
    )(*args)


def solution(mesh):
    row_spec = P(('batch', 'graph'), None)
    flat_spec = P(('batch', 'graph'))
    rep_spec = P(None, None)

    def device_step(grid_in, mesh_in, edge_in, edge_src, edge_dst, edge_mask, *rest):
        sizes = (grid_in.shape[0], mesh_in.shape[0], edge_in.shape[0], rest[1].shape[1], grid_in.shape[1])
        args = (grid_in.T, mesh_in.T, edge_in.T, edge_src[None], edge_dst[None], edge_mask[None]) + rest
        mesh_out, grid_out, ggrad, w1_grad, w2_grad = step_call(args, sizes)
        return mesh_out, grid_out, ggrad.T, w1_grad, w2_grad

    in_specs = (row_spec, row_spec, row_spec, flat_spec, flat_spec, flat_spec) + (rep_spec,) * 18 + (row_spec, row_spec)
    return jax.shard_map(device_step, mesh=mesh, in_specs=in_specs, out_specs=(row_spec,) * 5, check_vma=False)
```

time: 1010 us -> 149 us (0.15); the launches traced: 1000 us -> 149 us
  blocking collectives: 336 us -> 0 us
  other arithmetic: 165 us -> 0 us
  local copies, waits for them, and re-layouts: 165 us -> 5.55 us
  Pallas kernels: 0 us -> 143 us
  matrix products: 121 us -> 0 us
  starting transfers between devices: 105 us -> 0 us
  waiting for transfers between devices: 90.8 us -> 0 us
  between operations: 16 us -> 0.68 us
    unnamed x1 -> x0, blocking collectives: 336 us -> none
    pallas_call x0 -> x1, Pallas kernels: none -> 143 us  [step_call(): pl.pallas_call(step_kernel, out_shape=out_shape, in_specs=[pl.BlockSpec(m...]
    dot_general x17 -> x0, matrix products: 121 us -> none  [the longest x4 28.2 us: mlp_forward(): jnp.dot(x_in, w_one, preferred_element_type=jnp.float32) + vec_rows[0]]
    scatter-add x2 -> x0, other arithmetic: 111 us -> none  [the longest x1 61 us: device_step(): jax.ops.segment_sum(message, edge_dst, num_segments=mesh_rows)]
    gather x3 -> x0, local copies, waits for them, and re-layouts: 99.9 us -> none  [the longest x1 33.6 us: device_step(): row_table[local_src]]
    unnamed x33 -> x0, starting transfers between devices: 93.7 us -> none
    unnamed x34 -> x0, waiting for transfers between devices: 90.8 us -> none
    unnamed x124 -> x11, local copies, waits for them, and re-layouts: 61 us -> 5.55 us
  transfers between devices with their start and end apart: 37 -> 0, of which waited for: 1 -> 0; matrix products, arithmetic and copies ran while one was open for 21% -> 0% of each run, Pallas kernels for 0% -> 0%
where the time goes in v2:
time: 149 us
  Pallas kernels  143 us (96%)
  local copies, waits for them, and re-layouts  5.55 us (4%)
    pallas_call x1, Pallas kernels, step_call(): pl.pallas_call(step_kernel, out_shape=out_shape, in_specs=[pl.BlockSpec(m...  143 us
    unnamed x11, local copies, waits for them, and re-layouts  5.55 us

profile of v2, /device:TPU:1, one launch (start us, length us, event | category | flops | bytes accessed | tf_op | source)
XLA Modules:
  0.0 149.2 jit_solution(7539824582777991423)
XLA Ops:
  0.6 143.0 %whole_step.1 = (bf16[256,512]{1,0:T(8,128)(2,1)}, bf16[512,512]{1,0:T(8,128)(2,1)}, f32[186,512]{1,0:T(8,128)}, f32[12,512]{1,0:T(8,128)}, f32[4,512]{1,0:T(4,128)}) custom-call(f32[186,512]{1,0:T(8,128)} %bitcast.7, f32[3,256]{1,0:T(4,128)} %bitcast.13, f32[4,8192]{1,0:T(4,128)} %bitcast.9, s32[1,8192]{1,0:T(1,128)} %bitcast.10, s32[1,8192]{1,0:T(1,128)} %bitcast.11, ...), custom_call_target="tpu_custom_call" | custom-call | tf_op jit(solution)/shard_map/whole_step/pallas_call | solution.py:372
  143.6 0.0 copy-start
  143.6 0.0 copy-start.1
  143.6 0.0 copy-start.2
  143.7 1.7 %copy.36 = bf16[256,512]{1,0:T(8,128)(2,1)} copy(bf16[256,512]{1,0:T(8,128)(2,1)} %get-tuple-element.20) | data formatting | bytes 524288
  145.4 1.9 %copy.37 = bf16[512,512]{1,0:T(8,128)(2,1)} copy(bf16[512,512]{1,0:T(8,128)(2,1)} %get-tuple-element.21) | data formatting | bytes 1048576
  147.2 0.0 copy-done
  147.2 0.7 copy.38
  148.0 0.0 copy-done.1
  148.0 0.6 copy.39
  148.6 0.0 copy-done.2
  148.6 0.6 copy.40
Async XLA Ops:
  143.6 3.6 %copy-start = (f32[186,512]{1,0:T(8,128)S(1)}, f32[186,512]{1,0:T(8,128)}, u32[]{:S(2)}) copy-start(f32[186,512]{1,0:T(8,128)} %get-tuple-element.12) | copy-start | bytes 1142788
  143.6 4.4 %copy-start.1 = (f32[12,512]{1,0:T(8,128)S(1)}, f32[12,512]{1,0:T(8,128)}, u32[]{:S(2)}) copy-start(f32[12,512]{1,0:T(8,128)} %get-tuple-element.23) | copy-start | bytes 73732
  143.6 5.0 %copy-start.2 = (f32[4,512]{1,0:T(4,128)S(1)}, f32[4,512]{1,0:T(4,128)}, u32[]{:S(2)}) copy-start(f32[4,512]{1,0:T(4,128)} %get-tuple-element.24) | copy-start | bytes 24580
